TPU v7x, 32 devices: a whole 2x2x4 slice. The times are simulated.
32 devices in a mesh: dp: 8 (over y, x, core), mp: 4 (over z).
Axes of the slice: x: 2, y: 2, z: 4, core: 2. Of those that a mesh axis runs over, the one named last changes fastest.
Arguments:
- hidden_states: bfloat16 [16384, 4096], P('dp', 'mp'), may hold values from -1 to 1
- factor_values: bfloat16 [16384, 64], P('dp', 'mp'), may hold values from 0.029907227 to 0.13964844
- class_ids: int32 [16384, 64], P('dp', 'mp'), may hold values from 0 to 128255, as said below
- centers: int32 [3], replicated, may hold values from 0 to 16383
Outputs:
- min_distance: float32 [16384], P(('dp', 'mp'))
- weight_means: float32 [3], replicated
Inputs may be any that keep to these rules, and one draw needn't show every extreme that they name: `centers`: each value is a sample index. `class_ids`: entries k * 16 to (k + 1) * 16 - 1 of a row hold distinct classes of the k-th of 4 equal ranges of the vocabulary.
All inputs are finite; a program needn't handle non-finite values.
Results may differ from a plain program's by a relative error of at most 0.00095.
Values may be sent and summed in bfloat16 or wider, within the bound.
A program may use at most 64 MiB of HBM per device.

v0:
```python
import jax
import jax.numpy as jnp
from jax import lax
from jax.sharding import PartitionSpec as P

K_LOC = 16
STEPS = 3


def match_sum(idents, values, id_row, val_row):
    nblk = idents.shape[1] // K_LOC
    match = idents.reshape(-1, nblk, K_LOC, 1) == id_row.reshape(1, nblk, 1, K_LOC)
    prod = values.astype(jnp.float32).reshape(-1, nblk, K_LOC, 1) * val_row.astype(
        jnp.float32
    ).reshape(1, nblk, 1, K_LOC)
    return jnp.sum(jnp.where(match, prod, jnp.float32(0.0)), axis=(1, 2, 3))


def squares(values):
    return jnp.sum(jnp.square(values.astype(jnp.float32)), axis=1)


def body(hidden_states, factor_values, class_ids, centers):
    means = []
    min_distance = None
    rows_all = hidden_states.shape[0]
    rows = rows_all // lax.axis_size("mp")
    device_pos = lax.axis_index("dp")
    model_pos = lax.axis_index("mp")
    width_h = hidden_states.shape[1]
    width_a = factor_values.shape[1]
    start_h = model_pos * width_h
    start_a = model_pos * width_a
    full_h = width_h * lax.axis_size("mp")
    full_a = width_a * lax.axis_size("mp")
    owners = centers // rows_all
    offsets = centers - owners * rows_all
    mine = (owners == device_pos).astype(jnp.float32)[:, None]
    pick_h = hidden_states[offsets].astype(jnp.float32) * mine
    pick_v = factor_values[offsets].astype(jnp.float32) * mine
    pick_i = class_ids[offsets].astype(jnp.float32) * mine
    count = centers.shape[0]
    table_h = lax.dynamic_update_slice(
        jnp.zeros((count, full_h), jnp.float32), pick_h, (0, start_h)
    )
    table_v = lax.dynamic_update_slice(
        jnp.zeros((count, full_a), jnp.float32), pick_v, (0, start_a)
    )
    table_i = lax.dynamic_update_slice(
        jnp.zeros((count, full_a), jnp.float32), pick_i, (0, start_a)
    )
    table_h, table_v, table_i = lax.psum((table_h, table_v, table_i), ("dp", "mp"))
    center_hn = jnp.sum(table_h * table_h, axis=1)
    center_an = jnp.sum(table_v * table_v, axis=1)
    local_h = lax.dynamic_slice_in_dim(table_h, start_h, width_h, 1).astype(jnp.bfloat16)
    local_v = lax.dynamic_slice_in_dim(table_v, start_a, width_a, 1).astype(jnp.bfloat16)
    local_i = lax.dynamic_slice_in_dim(table_i, start_a, width_a, 1).astype(jnp.int32)
    prods_h = jnp.dot(hidden_states, local_h.T, preferred_element_type=jnp.float32)
    prods_a = [
        match_sum(class_ids, factor_values, local_i[step], local_v[step]) for step in range(STEPS)
    ]
    pieces = [squares(hidden_states), squares(factor_values)]
    pieces = pieces + [prods_h[:, step] for step in range(STEPS)] + prods_a
    summed = lax.psum_scatter(jnp.stack(pieces), "mp", scatter_dimension=1, tiled=True)
    sq_h = summed[0]
    sq_a = summed[1]
    pool_total = rows * lax.axis_size("dp") * lax.axis_size("mp")
    for step in range(STEPS):
        inner_h = summed[2 + step]
        inner_a = summed[2 + STEPS + step]
        norm_hc = center_hn[step]
        norm_ac = center_an[step]
        dist = jnp.maximum(
            sq_h * sq_a + norm_hc * norm_ac - 2.0 * inner_h * inner_a, jnp.float32(0.0)
        )
        min_distance = dist if step == 0 else jnp.minimum(min_distance, dist)
        total = lax.psum(jnp.sum(min_distance), ("dp", "mp"))
        means.append(total / pool_total)
    weight_means = jnp.stack(means)
    return (min_distance, weight_means)


def solution(mesh):
    return jax.shard_map(
        body,
        mesh=mesh,
        in_specs=(P("dp", "mp"), P("dp", "mp"), P("dp", "mp"), P()),
        out_specs=(P(("dp", "mp")), P()),
        check_vma=False,
    )
```

profile of v0, /device:TPU:0, one launch (start us, length us, event | category | flops | bytes accessed | tf_op | source)
XLA Modules:
  0.0 140.8 jit_solution(13213630061364509689)
XLA Ops:
  7.2 1.1 copy.11
  8.3 0.9 convert_element_type.61
  9.2 0.9 multiply_reduce_fusion.1
  10.1 0.7 compare_convert_fusion
  10.7 0.7 compare_select_fusion
  11.4 1.2 copy.10
  12.6 3.1 %multiply_reduce_fusion = f32[2048]{0:T(1024)S(1)} fusion(bf16[2048,1024]{1,0:T(8,128)(2,1)} %param.4), kind=kLoop, calls=%fused_computation.3 | loop fusion | flops 6289408 | bytes 4202496 | tf_op jit(solution)/shard_map/reduce_sum | solution.py:20
  15.7 3.3 %gather_fusion = bf16[3,1024]{1,0:T(4,128)(2,1)S(1)} fusion(bf16[2048,1024]{1,0:T(8,128)(2,1)} %param.4, s32[1024]{0:T(1024)S(1)} %pad_clamp_fusion), kind=kCustom, calls=%fused_computation | custom fusion | bytes 12300 | tf_op jit(solution)/shard_map/gather | solution.py:39
  19.0 0.6 gather_fusion.1
  19.6 0.6 gather_fusion.2
  20.3 0.1 dynamic_update_slice.11
  20.6 42.8 %all-reduce.1 = (f32[3,4096]{1,0:T(4,128)S(1)}, f32[3,64]{1,0:T(4,128)S(1)}, f32[3,64]{1,0:T(4,128)S(1)}) all-reduce(f32[3,4096]{1,0:T(4,128)S(1)} %multiply_dynamic-update-slice_fusion, f32[3,64]{1,0:T(4,128)S(1)} %dynamic_update_slice.11, f32[3,64]{1,0:T(4,128)S(1)} %dynamic_update_slice.10), channel_id=1, replica_groups=mesh['dp'=8,'mp'=4] {'dp','mp'}, use_global_device_ids=true, to_apply=%region_2.3 | all-reduce | flops 12672 | bytes 101376 | tf_op jit(solution)/shard_map/psum | solution.py:52
  63.6 3.4 %convolution_bitcast_fusion = f32[2048,3]{0,1:T(4,128)S(1)} fusion(bf16[2048,1024]{1,0:T(8,128)(2,1)} %param.4, f32[3,4096]{1,0:T(4,128)S(1)} %get-tuple-element.8, s32[]{:T(128)S(6)} %select_n.56), kind=kOutput, calls=%fused_computation.4 | convolution fusion | flops 12582912 | bytes 4227076 | tf_op jit(solution)/shard_map/dot_general | solution.py:58
  67.0 0.9 select_reduce_fusion
  67.9 0.7 stack.35
  68.7 0.1 multiply_reduce_fusion.2
  68.8 0.1 multiply_reduce_fusion.3
  68.9 0.7 fusion.9
  73.4 14.5 %reduce-scatter.2.cloned.1.call-done = f32[8,512]{1,0:T(8,128)} async-done(((f32[8,2048]{1,0:T(8,128)}), f32[8,512]{1,0:T(8,128)}) %reduce-scatter.2.cloned.1.call-update) | async-done | bytes 16400 | tf_op jit(solution)/shard_map/reduce_scatter | solution.py:64
  87.9 1.5 %fusion.5 = (f32[]{:T(128)}, f32[1,512]{1,0:T(1,128)S(1)}, f32[1,512]{1,0:T(1,128)S(1)}) fusion(f32[8,512]{1,0:T(8,128)} %reduce-scatter.2.cloned.1.call-done, f32[]{:T(128)} %bitcast.15), kind=kLoop, calls=%fused_computation.48 | loop fusion | flops 3583 | bytes 12296 | tf_op jit(solution)/shard_map/reduce_sum | solution.py:77
  89.4 1.4 fusion.7
  90.8 2.0 %fusion.8 = (f32[]{:T(128)}, f32[1,512]{1,0:T(1,128)}) fusion(f32[1,512]{1,0:T(1,128)S(1)} %get-tuple-element.15, f32[8,512]{1,0:T(8,128)} %reduce-scatter.2.cloned.1.call-done, f32[1,512]{1,0:T(1,128)S(1)} %get-tuple-element.13, f32[]{:T(128)} %bitcast.17), kind=kLoop, calls=%fused_computation.50 | loop fusion | flops 3583 | bytes 10248 | tf_op jit(solution)/shard_map/reduce_sum | solution.py:77
  92.8 38.6 %all-reduce = (f32[]{:T(128)}, f32[]{:T(128)}, f32[]{:T(128)}) all-reduce(f32[]{:T(128)} %get-tuple-element.16, f32[]{:T(128)} %get-tuple-element.14, f32[]{:T(128)} %get-tuple-element.11), channel_id=1, replica_groups=mesh['dp'=8,'mp'=4] {'dp','mp'}, use_global_device_ids=true, to_apply=%region_16.17 | all-reduce | flops 3 | bytes 24 | tf_op jit(solution)/shard_map/psum | solution.py:77
  133.4 0.6 pad_maximum_fusion
  (16 shorter events, 0.5 us)
Async XLA Ops:
  7.2 80.8 %reduce-scatter.2.cloned.1.call-start = ((), (), s32[]{:S(2)}) async-start(), calls=%async_computation.1 | async-start | bytes 81920 | tf_op jit(solution)/shard_map/reduce_scatter | solution.py:64
  63.6 3.4 %copy-start = (s32[2048,16]{0,1:T(8,128)S(1)}, s32[2048,16]{0,1:T(8,128)}, u32[]{:S(2)}) copy-start(s32[2048,16]{0,1:T(8,128)} %param.6) | copy-start | bytes 393220
Sparse Core Ops, SparseCore 0:
  68.8 19.0 reduce-scatter.1
where the time goes:
time: 142 us; the launch traced here: 141 us
  blocking collectives  81.4 us (57%)
  between operations  19.9 us (14%)
  waiting for transfers between devices  14.6 us (10%)
  other arithmetic  13 us (9%)
  local copies, waits for them, and re-layouts  8.53 us (6%)
  matrix products  3.4 us (2%)
    psum x1, blocking collectives, body(): lax.psum((table_h, table_v, table_i), ('dp', 'mp'))  42.8 us
    psum x1, blocking collectives, body(): total = lax.psum(jnp.sum(min_distance), ('dp', 'mp'))  38.6 us
    reduce_scatter x1, waiting for transfers between devices, body(): lax.psum_scatter(jnp.stack(pieces), 'mp', scatter_dimension=1, tiled=True)  14.5 us
    reduce_sum x3, other arithmetic, body(): total = lax.psum(jnp.sum(min_distance), ('dp', 'mp'))  4.89 us
    reduce_sum x2, other arithmetic, squares(): return jnp.sum(jnp.square(values.astype(jnp.float32)), axis=1)  3.95 us
    dot_general x1, matrix products, body(): jnp.dot(hidden_states, local_h.T, preferred_element_type=jnp.float32)  3.4 us
    gather x1, local copies, waits for them, and re-layouts, body(): pick_h = hidden_states[offsets].astype(jnp.float32) * mine  3.3 us
  transfers between devices with their start and end apart: 1, of which 1 were waited for; matrix products, arithmetic and copies ran while one was open for 1% of the time, Pallas kernels for 0%

commit v1 on v0

v1 whole, which is shorter than its diff:
```python
import functools

import jax
import jax.numpy as jnp
from jax import lax
from jax.experimental import pallas as pl
from jax.experimental.pallas import tpu as pltpu
from jax.sharding import PartitionSpec as P

MESH = pl.DeviceIdType.MESH
STEPS = 3
LANES = 128
TALL = 16
NT = (((1,), (1,)), ((), ()))


def kernel(
    DP, MP,
    c_ref, h_hbm, v_hbm, i_hbm,
    dist_ref, mean_ref,
    h, v, ids, ch_buf, meta_buf, ch_slots, meta_slots, part, part_slots, row_buf, row_slots,
    h_sem, i_sem, v_sem, a_send, a_recv, b_send, b_recv, c_send, c_recv, d_send, d_recv,
):
    groups, tall, width = h.shape
    rows = groups * tall
    tiles, depth, _ = ids.shape
    blk = rows // MP
    my_dp = lax.axis_index("dp")
    my_mp = lax.axis_index("mp")
    me = my_dp * MP + my_mp
    f32 = jnp.float32

    copies = [pltpu.make_async_copy(h_hbm, h, h_sem)]
    for j in range(tiles):
        at = pl.ds(j * LANES, LANES)
        copies.append(pltpu.make_async_copy(i_hbm.at[:, at], ids.at[j], i_sem.at[j]))
        copies.append(pltpu.make_async_copy(v_hbm.at[:, at], v.at[j], v_sem.at[j]))
    for copy in copies:
        copy.start()

    barrier = pltpu.get_barrier_semaphore()
    for d in range(1, DP):
        pl.semaphore_signal(
            barrier, inc=1, device_id=(lax.rem(my_dp + d, DP), my_mp), device_id_type=MESH
        )
    for d in range(1, MP):
        pl.semaphore_signal(
            barrier, inc=1, device_id=(my_dp, lax.rem(my_mp + d, MP)), device_id_type=MESH
        )
    for copy in copies:
        copy.wait()

    lane = lax.broadcasted_iota(jnp.int32, (2 * depth, LANES), 1)
    row16 = lax.broadcasted_iota(jnp.int32, (tall, 1), 0)
    picks = []
    meta = jnp.zeros((2 * depth, LANES), f32)
    for t in range(STEPS):
        c = c_ref[t]
        off = lax.rem(c, rows)
        g = lax.div(off, tall)
        tile = h[g].astype(f32)
        hit = row16 + (my_dp * rows + g * tall) == c
        picks.append(jnp.sum(jnp.where(hit, tile, 0.0), axis=0, keepdims=True))
        g = lax.div(off, LANES)
        both = jnp.concatenate([ids[g].astype(f32), v[g].astype(f32)], axis=0)
        lhit = lane + (my_dp * rows + g * LANES) == c
        col = jnp.sum(jnp.where(lhit, both, 0.0), axis=1, keepdims=True)
        meta = jnp.where(lane == t, col, meta)
    picks.append(jnp.zeros((1, width), f32))
    ch_buf[...] = jnp.concatenate(picks, axis=0).astype(jnp.bfloat16)
    wide = jnp.concatenate([meta, jnp.zeros((LANES - 2 * depth, LANES), f32)], axis=0)
    meta_buf[...] = wide.T[0:8, :]

    pl.semaphore_wait(barrier, DP - 1 + MP - 1)
    sends = []
    for d in range(1, DP):
        to = (lax.rem(my_dp + d, DP), my_mp)
        for src, dst, ss, rs in (
            (ch_buf, ch_slots, a_send, a_recv),
            (meta_buf, meta_slots, b_send, b_recv),
        ):
            copy = pltpu.make_async_remote_copy(
                src_ref=src, dst_ref=dst.at[d - 1],
                send_sem=ss.at[d - 1], recv_sem=rs.at[d - 1],
                device_id=to, device_id_type=MESH,
            )
            copy.start()
            sends.append(copy)

    ones = jnp.ones((8, LANES), jnp.bfloat16)
    for b in range(MP):
        y = jnp.zeros((blk // tall, tall, LANES), f32)
        for j in range(width // LANES):
            x = h[b * blk // tall:(b + 1) * blk // tall, :, j * LANES:(j + 1) * LANES].astype(f32)
            y = y + x * x
        y = y.reshape(blk, LANES)
        hi = y.astype(jnp.bfloat16)
        lo = (y - hi.astype(f32)).astype(jnp.bfloat16)
        sq = lax.dot_general(ones, hi, NT, preferred_element_type=f32)
        sq = sq + lax.dot_general(ones, lo, NT, preferred_element_type=f32)
        part[b, 3:4, 0:blk] = sq[0:1]
        for j in range(blk // LANES):
            a = v[b * blk // LANES + j].astype(f32)
            part[b, 7:8, j * LANES:(j + 1) * LANES] = jnp.sum(a * a, axis=0, keepdims=True)

    for copy in sends:
        copy.wait_recv()
    ch4 = ch_buf[...].astype(f32)
    cm = meta_buf[...]
    for d in range(DP - 1):
        ch4 = ch4 + ch_slots[d].astype(f32)
        cm = cm + meta_slots[d]
    ch = jnp.concatenate([ch4, jnp.zeros_like(ch4)], axis=0).astype(jnp.bfloat16)
    nh = jnp.sum(ch4 * ch4, axis=1, keepdims=True)
    lane8 = lax.broadcasted_iota(jnp.int32, (8, LANES), 1)
    na = jnp.sum(jnp.where(lane8 >= depth, cm * cm, 0.0), axis=1, keepdims=True)
    norms = jnp.broadcast_to(jnp.concatenate([nh, na[0:4]], axis=0), (8, LANES))
    cols = jnp.concatenate([cm, jnp.zeros((LANES - 8, LANES), f32)], axis=0).T
    id_cols = [
        jnp.broadcast_to(cols[0:depth, t:t + 1], (depth, LANES)).astype(jnp.int32)
        for t in range(STEPS)
    ]
    v_cols = [
        jnp.broadcast_to(cols[depth:2 * depth, t:t + 1], (depth, LANES)) for t in range(STEPS)
    ]

    outs = []
    for d in list(range(1, MP)) + [0]:
        b = lax.rem(my_mp + d, MP)
        hb = h[pl.ds(b * (blk // tall), blk // tall)].reshape(blk, width)
        hh = lax.dot_general(ch, hb, NT, preferred_element_type=f32)
        part[b, 0:STEPS, 0:blk] = hh[0:STEPS]
        part[b, :, blk:] = norms
        for j in range(blk // LANES):
            bid = ids[b * (blk // LANES) + j]
            bv = v[b * (blk // LANES) + j].astype(f32)
            for t in range(STEPS):
                w = jnp.zeros((depth, LANES), f32)
                for l in range(depth):
                    w = jnp.where(bid == id_cols[t][l:l + 1], v_cols[t][l:l + 1], w)
                part[b, 4 + t:5 + t, j * LANES:(j + 1) * LANES] = jnp.sum(
                    bv * w, axis=0, keepdims=True
                )
        if d:
            copy = pltpu.make_async_remote_copy(
                src_ref=part.at[b], dst_ref=part_slots.at[d - 1],
                send_sem=c_send.at[d - 1], recv_sem=c_recv.at[d - 1],
                device_id=(my_dp, b), device_id_type=MESH,
            )
            copy.start()
            outs.append(copy)
    total = part[my_mp]
    for d, copy in enumerate(outs):
        copy.wait_recv()
        total = total + part_slots[d]

    pq = total[0:4] * total[4:8]
    lane1 = lax.broadcasted_iota(jnp.int32, (1, LANES), 1)
    own = pq[3:4, 0:blk]
    row = jnp.zeros((1, LANES), f32)
    low = None
    for t in range(STEPS):
        center = jnp.concatenate([pq[t:t + 1, blk:]] * (blk // LANES), axis=1)
        dist = jnp.maximum(own + center - 2.0 * pq[t:t + 1, 0:blk], 0.0)
        low = dist if low is None else jnp.minimum(low, dist)
        row = jnp.where(lane1 == t, jnp.sum(low, axis=1, keepdims=True), row)
    row_buf[...] = row
    lasts = []
    for d in range(1, DP * MP):
        to = lax.rem(me + d, DP * MP)
        copy = pltpu.make_async_remote_copy(
            src_ref=row_buf, dst_ref=row_slots.at[pl.ds(me, 1)],
            send_sem=d_send.at[d - 1], recv_sem=d_recv.at[d - 1],
            device_id=(lax.div(to, MP), lax.rem(to, MP)), device_id_type=MESH,
        )
        copy.start()
        lasts.append(copy)
    row_slots[pl.ds(me, 1), :] = row
    dist_ref[...] = low
    for copy in sends + outs:
        copy.wait_send()
    for copy in lasts:
        copy.wait()
    mean_ref[...] = jnp.sum(row_slots[...], axis=0, keepdims=True) / (blk * MP * DP)


def solution(mesh):
    DP, MP = mesh.shape["dp"], mesh.shape["mp"]

    def body(hidden_states, factor_values, class_ids, centers):
        rows, width = hidden_states.shape
        depth = class_ids.shape[1]
        blk = rows // MP
        vm = pltpu.VMEM
        sem = pltpu.SemaphoreType.DMA
        hbm = pl.BlockSpec(memory_space=pl.ANY)
        low, mean = pl.pallas_call(
            functools.partial(kernel, DP, MP),
            out_shape=(
                jax.ShapeDtypeStruct((1, blk), jnp.float32),
                jax.ShapeDtypeStruct((1, LANES), jnp.float32),
            ),
            in_specs=[pl.BlockSpec(memory_space=pltpu.SMEM), hbm, hbm, hbm],
            out_specs=(pl.BlockSpec(memory_space=vm), pl.BlockSpec(memory_space=vm)),
            scratch_shapes=[
                vm((rows // TALL, TALL, width), jnp.bfloat16),
                vm((rows // LANES, depth, LANES), jnp.bfloat16),
                vm((rows // LANES, depth, LANES), jnp.int32),
                vm((4, width), jnp.bfloat16),
                vm((8, LANES), jnp.float32),
                vm((DP - 1, 4, width), jnp.bfloat16),
                vm((DP - 1, 8, LANES), jnp.float32),
                vm((MP, 8, blk + LANES), jnp.float32),
                vm((MP - 1, 8, blk + LANES), jnp.float32),
                vm((1, LANES), jnp.float32),
                vm((DP * MP, LANES), jnp.float32),
                sem, sem((rows // LANES,)), sem((rows // LANES,)),
                sem((DP - 1,)), sem((DP - 1,)), sem((DP - 1,)), sem((DP - 1,)),
                sem((MP - 1,)), sem((MP - 1,)),
                sem((DP * MP - 1,)), sem((DP * MP - 1,)),
            ],
            compiler_params=pltpu.CompilerParams(collective_id=0, has_side_effects=True),
        )(centers, hidden_states.reshape(rows // TALL, TALL, width), factor_values.T, class_ids.T)
        return low.reshape(blk), mean[0, :STEPS]

    return jax.shard_map(
        body,
        mesh=mesh,
        in_specs=(P("dp", "mp"), P("dp", "mp"), P("dp", "mp"), P()),
        out_specs=(P(("dp", "mp")), P()),
        check_vma=False,
    )
```

time: 142 us -> 23.8 us (0.17)
  blocking collectives: 81.4 us -> 0 us
  Pallas kernels: 0 us -> 20.6 us
  between operations: 19.9 us -> 0.64 us
  waiting for transfers between devices: 14.6 us -> 0 us
  other arithmetic: 13 us -> 0 us
  local copies, waits for them, and re-layouts: 8.53 us -> 2.39 us
  matrix products: 3.4 us -> 0 us
    psum x2 -> x0, blocking collectives: 81.4 us -> none  [the longest x1 42.8 us: body(): lax.psum((table_h, table_v, table_i), ('dp', 'mp'))]
    pallas_call x0 -> x1, Pallas kernels: none -> 20.6 us  [body(): pl.pallas_call(functools.partial(kernel, DP, MP), out_shape=(jax.ShapeDty...]
    reduce_scatter x1 -> x0, waiting for transfers between devices: 14.5 us -> none  [body(): lax.psum_scatter(jnp.stack(pieces), 'mp', scatter_dimension=1, tiled=True)]
    reduce_sum x8 -> x0, other arithmetic: 10 us -> none  [the longest x3 4.89 us: body(): total = lax.psum(jnp.sum(min_distance), ('dp', 'mp'))]
    gather x3 -> x0, local copies, waits for them, and re-layouts: 4.42 us -> none  [the longest x1 3.3 us: body(): pick_h = hidden_states[offsets].astype(jnp.float32) * mine]
    dot_general x1 -> x0, matrix products: 3.4 us -> none  [body(): jnp.dot(hidden_states, local_h.T, preferred_element_type=jnp.float32)]
    convert_element_type x4 -> x0, other arithmetic: 1.6 us -> none  [the longest x1 0.85 us: squares(): return jnp.sum(jnp.square(values.astype(jnp.float32)), axis=1)]
  transfers between devices with their start and end apart: 1 -> 0, of which waited for: 1 -> 0; matrix products, arithmetic and copies ran while one was open for 1% -> 0% of each run, Pallas kernels for 0% -> 0%
where the time goes in v1:
time: 23.8 us; the launch traced here: 23.6 us
  Pallas kernels  20.6 us (87%)
  local copies, waits for them, and re-layouts  2.39 us (10%)
  between operations  0.64 us (3%)
    pallas_call x1, Pallas kernels, body(): pl.pallas_call(functools.partial(kernel, DP, MP), out_shape=(jax.ShapeDty...  20.6 us
    unnamed x1, local copies, waits for them, and re-layouts  1.25 us
    squeeze x1, local copies, waits for them, and re-layouts, body(): return (low.reshape(blk), mean[0, :STEPS])  1.14 us

profile of v1, /device:TPU:0, one launch (start us, length us, event | category | flops | bytes accessed | tf_op | source)
XLA Modules:
  0.0 23.6 jit_solution(15094006233224777992)
XLA Ops:
  0.6 20.6 %shard_map.59 = (f32[1,512]{1,0:T(1,128)}, f32[1,128]{1,0:T(1,128)}) custom-call(s32[3]{0:T(128)} %c_ref.1, bf16[128,16,1024]{2,1,0:T(8,128)(2,1)} %bitcast.6, bf16[16,2048]{1,0:T(8,128)(2,1)} %bitcast.8, s32[16,2048]{1,0:T(8,128)} %bitcast.7), custom_call_target="tpu_custom_call" | custom-call | tf_op jit(solution)/shard_map/pallas_call | solution.py:197
  21.2 1.1 %slice_bitcast_fusion = f32[3]{0:T(128)} fusion(f32[1,128]{1,0:T(1,128)} %get-tuple-element.5), kind=kLoop, calls=%fused_computation | loop fusion | bytes 24 | tf_op jit(solution)/shard_map/squeeze | solution.py:224
  22.3 1.2 %copy.7 = f32[512]{0:T(512)} copy(f32[512]{0:T(512)} %bitcast.9) | data formatting | bytes 4096

commit v2 on v1

v2 whole, which is shorter than its diff:
```python
import functools

import jax
import jax.numpy as jnp
from jax import lax
from jax.experimental import pallas as pl
from jax.experimental.pallas import tpu as pltpu
from jax.sharding import PartitionSpec as P

MESH = pl.DeviceIdType.MESH
STEPS = 3
LANES = 128
TALL = 16
NT = (((1,), (1,)), ((), ()))


def partner(p, k, n):
    if n & (n - 1):
        return lax.rem(p + k, n)
    bit = 1
    q = p
    while bit <= k:
        if k & bit:
            q = q + bit - 2 * bit * lax.rem(lax.div(p, bit), 2)
        bit *= 2
    return q


def kernel(
    DP, MP,
    c_hbm, h_hbm, v_hbm, i_hbm,
    dist_ref, mean_ref,
    c_ref, h, v, ids, ch_buf, ch_slots, sq, sq_slots, norm_buf, norm_slots, part, part_slots,
    row_buf, row_slots,
    z_sem, h_sem, i_sem, v_sem, a_send, a_recv, s_send, s_recv, n_send, n_recv, b_send, b_recv,
    d_send, d_recv,
):
    groups, tall, width = h.shape
    rows = groups * tall
    tiles, depth, _ = ids.shape
    blk = rows // MP
    my_dp = lax.axis_index("dp")
    my_mp = lax.axis_index("mp")
    me = my_dp * MP + my_mp
    f32 = jnp.float32

    copies = [
        pltpu.make_async_copy(c_hbm, c_ref, z_sem), pltpu.make_async_copy(h_hbm, h, h_sem)
    ]
    for j in range(tiles):
        at = pl.ds(j * LANES, LANES)
        copies.append(pltpu.make_async_copy(i_hbm.at[:, at], ids.at[j], i_sem.at[j]))
        copies.append(pltpu.make_async_copy(v_hbm.at[:, at], v.at[j], v_sem.at[j]))
    for copy in copies:
        copy.start()

    barrier = pltpu.get_barrier_semaphore()
    for d in range(1, DP):
        pl.semaphore_signal(
            barrier, inc=1, device_id=(lax.rem(my_dp + d, DP), my_mp), device_id_type=MESH
        )
    for d in range(1, MP):
        pl.semaphore_signal(
            barrier, inc=1, device_id=(my_dp, lax.rem(my_mp + d, MP)), device_id_type=MESH
        )
    for copy in copies:
        copy.wait()

    lane = lax.broadcasted_iota(jnp.int32, (4 * depth, LANES), 1)
    row16 = lax.broadcasted_iota(jnp.int32, (tall, 1), 0)
    picks = []
    meta = jnp.zeros((4 * depth, LANES), f32)
    for t in range(STEPS):
        c = c_ref[t]
        off = lax.rem(c, rows)
        g = lax.div(off, tall)
        tile = h[g].astype(f32)
        hit = row16 + (my_dp * rows + g * tall) == c
        picks.append(jnp.sum(jnp.where(hit, tile, 0.0), axis=0, keepdims=True))
        g = lax.div(off, LANES)
        k = ids[g]
        digits = [(k >> 12).astype(f32), ((k >> 6) & 63).astype(f32), (k & 63).astype(f32)]
        both = jnp.concatenate(digits + [v[g].astype(f32)], axis=0)
        lhit = lane + (my_dp * rows + g * LANES) == c
        col = jnp.sum(jnp.where(lhit, both, 0.0), axis=1, keepdims=True)
        meta = jnp.where(lane == t, col, meta)
    wide = jnp.concatenate([meta, jnp.zeros((LANES - 4 * depth, LANES), f32)], axis=0).T
    tail = [wide[t:t + 1] for t in range(STEPS)] + [jnp.zeros((1, width - STEPS * LANES), f32)]
    picks.append(jnp.concatenate(tail, axis=1))
    ch_buf[...] = jnp.concatenate(picks, axis=0).astype(jnp.bfloat16)

    pl.semaphore_wait(barrier, DP - 1 + MP - 1)
    sends = []
    for d in range(1, DP):
        copy = pltpu.make_async_remote_copy(
            src_ref=ch_buf, dst_ref=ch_slots.at[d - 1],
            send_sem=a_send.at[d - 1], recv_sem=a_recv.at[d - 1],
            device_id=(lax.rem(my_dp + d, DP), my_mp), device_id_type=MESH,
        )
        copy.start()
        sends.append(copy)

    ones = jnp.ones((8, LANES), jnp.bfloat16)
    for b in range(MP):
        y = jnp.zeros((blk // tall, tall, LANES), f32)
        for j in range(width // LANES):
            x = h[b * blk // tall:(b + 1) * blk // tall, :, j * LANES:(j + 1) * LANES].astype(f32)
            y = y + x * x
        y = y.reshape(blk, LANES)
        hi = y.astype(jnp.bfloat16)
        lo = (y - hi.astype(f32)).astype(jnp.bfloat16)
        norm = lax.dot_general(ones, hi, NT, preferred_element_type=f32)
        norm = norm + lax.dot_general(ones, lo, NT, preferred_element_type=f32)
        sq[b, 0:1] = norm[0:1]
        for j in range(blk // LANES):
            a = v[b * blk // LANES + j].astype(f32)
            sq[b, 1:2, j * LANES:(j + 1) * LANES] = jnp.sum(a * a, axis=0, keepdims=True)
    order = [(k, partner(my_mp, k, MP)) for k in reversed(range(1, MP))]
    early = []
    for k, b in order:
        copy = pltpu.make_async_remote_copy(
            src_ref=sq.at[b], dst_ref=sq_slots.at[k - 1],
            send_sem=s_send.at[k - 1], recv_sem=s_recv.at[k - 1],
            device_id=(my_dp, b), device_id_type=MESH,
        )
        copy.start()
        early.append(copy)

    for copy in sends:
        copy.wait_recv()
    ch4 = ch_buf[...].astype(f32)
    for d in range(DP - 1):
        ch4 = ch4 + ch_slots[d].astype(f32)
    ch = jnp.concatenate([ch4, jnp.zeros_like(ch4)], axis=0).astype(jnp.bfloat16)
    cm = jnp.concatenate(
        [ch4[3:4, t * LANES:(t + 1) * LANES] for t in range(STEPS)]
        + [jnp.zeros((LANES - STEPS, LANES), f32)],
        axis=0,
    )
    nh = jnp.sum(ch4 * ch4, axis=1, keepdims=True)
    lane8 = lax.broadcasted_iota(jnp.int32, (8, LANES), 1)
    cm8 = jnp.where(lane8 >= 3 * depth, cm[0:8], 0.0)
    na = jnp.sum(cm8 * cm8, axis=1, keepdims=True)
    lane1 = lax.broadcasted_iota(jnp.int32, (1, LANES), 1)
    norms = jnp.zeros((1, LANES), f32)
    for t in range(STEPS):
        norms = jnp.where(lane1 == t, nh[t:t + 1], norms)
        norms = jnp.where(lane1 == STEPS + t, na[t:t + 1], norms)
    norm_buf[...] = norms
    for k, b in order:
        copy = pltpu.make_async_remote_copy(
            src_ref=norm_buf, dst_ref=norm_slots.at[k - 1],
            send_sem=n_send.at[k - 1], recv_sem=n_recv.at[k - 1],
            device_id=(my_dp, b), device_id_type=MESH,
        )
        copy.start()
        early.append(copy)
    cols = cm.T
    id_cols, v_cols = [], []
    for t in range(STEPS):
        col = jnp.broadcast_to(cols[0:4 * depth, t:t + 1], (4 * depth, LANES))
        code = col[0:depth] * 4096.0 + col[depth:2 * depth] * 64.0 + col[2 * depth:3 * depth]
        id_cols.append(code.astype(jnp.int32))
        v_cols.append(col[3 * depth:])

    outs = []
    for d, b in order + [(0, my_mp)]:
        hb = h[pl.ds(b * (blk // tall), blk // tall)].reshape(blk, width)
        hh = lax.dot_general(ch, hb, NT, preferred_element_type=f32)
        part[b, 0:STEPS] = hh[0:STEPS]
        for j in range(blk // LANES):
            bid = ids[b * (blk // LANES) + j]
            bv = v[b * (blk // LANES) + j].astype(f32)
            for t in range(STEPS):
                w = jnp.zeros((depth, LANES), f32)
                for l in range(depth):
                    w = jnp.where(bid == id_cols[t][l:l + 1], v_cols[t][l:l + 1], w)
                part[b, STEPS + t:STEPS + t + 1, j * LANES:(j + 1) * LANES] = jnp.sum(
                    bv * w, axis=0, keepdims=True
                )
        if d:
            copy = pltpu.make_async_remote_copy(
                src_ref=part.at[b], dst_ref=part_slots.at[d - 1],
                send_sem=b_send.at[d - 1], recv_sem=b_recv.at[d - 1],
                device_id=(my_dp, b), device_id_type=MESH,
            )
            copy.start()
            outs.append(copy)
    own, norms, total = sq[my_mp], norm_buf[...], part[my_mp]
    for copy in early + outs:
        copy.wait_recv()
    for k in range(MP - 1):
        own = own + sq_slots[k]
        norms = norms + norm_slots[k]
        total = total + part_slots[k]

    own = own[0:1] * own[1:2]
    row = jnp.zeros((1, LANES), f32)
    low = None
    for t in range(STEPS):
        center = norms[:, t:t + 1] * norms[:, STEPS + t:STEPS + t + 1]
        cross = total[t:t + 1] * total[STEPS + t:STEPS + t + 1]
        dist = jnp.maximum(own + center - 2.0 * cross, 0.0)
        low = dist if low is None else jnp.minimum(low, dist)
        row = jnp.where(lane1 == t, jnp.sum(low, axis=1, keepdims=True), row)
    row_buf[...] = row
    lasts = []
    for d in range(1, DP * MP):
        to = lax.rem(me + d, DP * MP)
        copy = pltpu.make_async_remote_copy(
            src_ref=row_buf, dst_ref=row_slots.at[pl.ds(me, 1)],
            send_sem=d_send.at[d - 1], recv_sem=d_recv.at[d - 1],
            device_id=(lax.div(to, MP), lax.rem(to, MP)), device_id_type=MESH,
        )
        copy.start()
        lasts.append(copy)
    row_slots[pl.ds(me, 1), :] = row
    dist_ref[...] = low
    for copy in sends + early + outs:
        copy.wait_send()
    for copy in lasts:
        copy.wait()
    mean_ref[...] = jnp.sum(row_slots[...], axis=0, keepdims=True) / (blk * MP * DP)


def solution(mesh):
    DP, MP = mesh.shape["dp"], mesh.shape["mp"]

    def body(hidden_states, factor_values, class_ids, centers):
        rows, width = hidden_states.shape
        depth = class_ids.shape[1]
        blk = rows // MP
        vm = pltpu.VMEM
        sem = pltpu.SemaphoreType.DMA
        hbm = pl.BlockSpec(memory_space=pl.ANY)
        low, mean = pl.pallas_call(
            functools.partial(kernel, DP, MP),
            out_shape=(vm((1, blk), jnp.float32), vm((1, LANES), jnp.float32)),
            in_specs=[hbm] * 4,
            out_specs=(pl.BlockSpec(memory_space=vm), pl.BlockSpec(memory_space=vm)),
            scratch_shapes=[
                pltpu.SMEM((STEPS,), jnp.int32),
                vm((rows // TALL, TALL, width), jnp.bfloat16),
                vm((rows // LANES, depth, LANES), jnp.bfloat16),
                vm((rows // LANES, depth, LANES), jnp.int32),
                vm((4, width), jnp.bfloat16),
                vm((DP - 1, 4, width), jnp.bfloat16),
                vm((MP, 2, blk), jnp.float32),
                vm((MP - 1, 2, blk), jnp.float32),
                vm((1, LANES), jnp.float32),
                vm((MP - 1, 1, LANES), jnp.float32),
                vm((MP, 2 * STEPS, blk), jnp.float32),
                vm((MP - 1, 2 * STEPS, blk), jnp.float32),
                vm((1, LANES), jnp.float32),
                vm((DP * MP, LANES), jnp.float32),
                sem, sem, sem((rows // LANES,)), sem((rows // LANES,)),
                sem((DP - 1,)), sem((DP - 1,)),
                sem((MP - 1,)), sem((MP - 1,)),
                sem((MP - 1,)), sem((MP - 1,)),
                sem((MP - 1,)), sem((MP - 1,)),
                sem((DP * MP - 1,)), sem((DP * MP - 1,)),
            ],
            compiler_params=pltpu.CompilerParams(collective_id=0, has_side_effects=True),
        )(centers, hidden_states.reshape(rows // TALL, TALL, width), factor_values.T, class_ids.T)
        return low.reshape(blk), mean[0, :STEPS]

    return jax.shard_map(
        body,
        mesh=mesh,
        in_specs=(P("dp", "mp"), P("dp", "mp"), P("dp", "mp"), P()),
        out_specs=(P(("dp", "mp")), P()),
        check_vma=False,
    )
```

time: 23.8 us -> 20.5 us (0.86)
  Pallas kernels: 20.6 us -> 18.7 us
  local copies, waits for them, and re-layouts: 2.39 us -> 1.09 us
    pallas_call x1, Pallas kernels: 20.6 us -> 18.7 us  [body(): pl.pallas_call(functools.partial(kernel, DP, MP), out_shape=(vm((1, blk),...]
    unnamed x1, local copies, waits for them, and re-layouts: 1.25 us -> 0.58 us
    squeeze x1, local copies, waits for them, and re-layouts: 1.14 us -> 0.51 us  [body(): return (low.reshape(blk), mean[0, :STEPS])]
where the time goes in v2:
time: 20.5 us; the launch traced here: 20.4 us
  Pallas kernels  18.7 us (91%)
  local copies, waits for them, and re-layouts  1.09 us (5%)
  between operations  0.64 us (3%)
    pallas_call x1, Pallas kernels, body(): pl.pallas_call(functools.partial(kernel, DP, MP), out_shape=(vm((1, blk),...  18.7 us
    unnamed x1, local copies, waits for them, and re-layouts  0.58 us
    squeeze x1, local copies, waits for them, and re-layouts, body(): return (low.reshape(blk), mean[0, :STEPS])  0.51 us

profile of v2, /device:TPU:0, one launch (start us, length us, event | category | flops | bytes accessed | tf_op | source)
XLA Modules:
  0.0 20.4 jit_solution(17494506945723528273)
XLA Ops:
  0.6 18.7 %shard_map.59 = (f32[1,512]{1,0:T(1,128)S(1)}, f32[1,128]{1,0:T(1,128)S(1)}) custom-call(s32[3]{0:T(128)} %c_hbm.1, bf16[128,16,1024]{2,1,0:T(8,128)(2,1)} %bitcast.7, bf16[16,2048]{1,0:T(8,128)(2,1)} %bitcast.9, s32[16,2048]{1,0:T(8,128)} %bitcast.8), custom_call_target="tpu_custom_call" | custom-call | tf_op jit(solution)/shard_map/pallas_call | solution.py:236
  19.3 0.6 %copy.7 = f32[512]{0:T(512)} copy(f32[512]{0:T(512)S(1)} %bitcast.6) | data formatting | bytes 4096
  19.9 0.5 %slice_bitcast_fusion = f32[3]{0:T(128)} fusion(f32[1,128]{1,0:T(1,128)S(1)} %get-tuple-element.5), kind=kLoop, calls=%fused_computation | loop fusion | bytes 24 | tf_op jit(solution)/shard_map/squeeze | solution.py:265

commit v3 on v2

--- a/solution.py
+++ b/solution.py
@@ -11,6 +11,7 @@
 STEPS = 3
 LANES = 128
 TALL = 16
+CHUNKS = 8
 NT = (((1,), (1,)), ((), ()))
 
 
@@ -24,6 +25,10 @@
             q = q + bit - 2 * bit * lax.rem(lax.div(p, bit), 2)
         bit *= 2
     return q
+
+
+def drain(ref, sem):
+    pltpu.make_async_copy(ref, ref, sem).wait()
 
 
 def kernel(
@@ -43,16 +48,18 @@
     my_mp = lax.axis_index("mp")
     me = my_dp * MP + my_mp
     f32 = jnp.float32
-
-    copies = [
-        pltpu.make_async_copy(c_hbm, c_ref, z_sem), pltpu.make_async_copy(h_hbm, h, h_sem)
-    ]
+    dp_peers = [partner(my_dp, k, DP) for k in range(DP)]
+    mp_peers = [partner(my_mp, k, MP) for k in range(MP)]
+
+    pltpu.make_async_copy(c_hbm, c_ref, z_sem).start()
+    step = max(groups // CHUNKS, 1)
+    for j in range(0, groups, step):
+        at = pl.ds(j, step)
+        pltpu.make_async_copy(h_hbm.at[at], h.at[at], h_sem).start()
     for j in range(tiles):
         at = pl.ds(j * LANES, LANES)
-        copies.append(pltpu.make_async_copy(i_hbm.at[:, at], ids.at[j], i_sem.at[j]))
-        copies.append(pltpu.make_async_copy(v_hbm.at[:, at], v.at[j], v_sem.at[j]))
-    for copy in copies:
-        copy.start()
+        pltpu.make_async_copy(i_hbm.at[:, at], ids.at[j], i_sem).start()
+        pltpu.make_async_copy(v_hbm.at[:, at], v.at[j], v_sem).start()
 
     barrier = pltpu.get_barrier_semaphore()
     for d in range(1, DP):
@@ -63,42 +70,40 @@
         pl.semaphore_signal(
             barrier, inc=1, device_id=(my_dp, lax.rem(my_mp + d, MP)), device_id_type=MESH
         )
-    for copy in copies:
-        copy.wait()
+    pltpu.make_async_copy(c_hbm, c_ref, z_sem).wait()
+    drain(ids, i_sem)
+    drain(v, v_sem)
 
     lane = lax.broadcasted_iota(jnp.int32, (4 * depth, LANES), 1)
     row16 = lax.broadcasted_iota(jnp.int32, (tall, 1), 0)
-    picks = []
+    first = my_dp * rows
+    offs = [lax.rem(c_ref[t], rows) for t in range(STEPS)]
     meta = jnp.zeros((4 * depth, LANES), f32)
     for t in range(STEPS):
-        c = c_ref[t]
-        off = lax.rem(c, rows)
-        g = lax.div(off, tall)
-        tile = h[g].astype(f32)
-        hit = row16 + (my_dp * rows + g * tall) == c
-        picks.append(jnp.sum(jnp.where(hit, tile, 0.0), axis=0, keepdims=True))
-        g = lax.div(off, LANES)
+        g = lax.div(offs[t], LANES)
         k = ids[g]
         digits = [(k >> 12).astype(f32), ((k >> 6) & 63).astype(f32), (k & 63).astype(f32)]
         both = jnp.concatenate(digits + [v[g].astype(f32)], axis=0)
-        lhit = lane + (my_dp * rows + g * LANES) == c
-        col = jnp.sum(jnp.where(lhit, both, 0.0), axis=1, keepdims=True)
+        hit = lane + (first + g * LANES) == c_ref[t]
+        col = jnp.sum(jnp.where(hit, both, 0.0), axis=1, keepdims=True)
         meta = jnp.where(lane == t, col, meta)
     wide = jnp.concatenate([meta, jnp.zeros((LANES - 4 * depth, LANES), f32)], axis=0).T
+    drain(h, h_sem)
+    picks = []
+    for t in range(STEPS):
+        g = lax.div(offs[t], tall)
+        hit = row16 + (first + g * tall) == c_ref[t]
+        picks.append(jnp.sum(jnp.where(hit, h[g].astype(f32), 0.0), axis=0, keepdims=True))
     tail = [wide[t:t + 1] for t in range(STEPS)] + [jnp.zeros((1, width - STEPS * LANES), f32)]
     picks.append(jnp.concatenate(tail, axis=1))
     ch_buf[...] = jnp.concatenate(picks, axis=0).astype(jnp.bfloat16)
 
     pl.semaphore_wait(barrier, DP - 1 + MP - 1)
-    sends = []
-    for d in range(1, DP):
-        copy = pltpu.make_async_remote_copy(
-            src_ref=ch_buf, dst_ref=ch_slots.at[d - 1],
-            send_sem=a_send.at[d - 1], recv_sem=a_recv.at[d - 1],
-            device_id=(lax.rem(my_dp + d, DP), my_mp), device_id_type=MESH,
-        )
-        copy.start()
-        sends.append(copy)
+    for k in reversed(range(1, DP)):
+        pltpu.make_async_remote_copy(
+            src_ref=ch_buf, dst_ref=ch_slots.at[k - 1], send_sem=a_send, recv_sem=a_recv,
+            device_id=(dp_peers[k], my_mp), device_id_type=MESH,
+        ).start()
 
     ones = jnp.ones((8, LANES), jnp.bfloat16)
     for b in range(MP):
@@ -115,19 +120,13 @@
         for j in range(blk // LANES):
             a = v[b * blk // LANES + j].astype(f32)
             sq[b, 1:2, j * LANES:(j + 1) * LANES] = jnp.sum(a * a, axis=0, keepdims=True)
-    order = [(k, partner(my_mp, k, MP)) for k in reversed(range(1, MP))]
-    early = []
-    for k, b in order:
-        copy = pltpu.make_async_remote_copy(
-            src_ref=sq.at[b], dst_ref=sq_slots.at[k - 1],
-            send_sem=s_send.at[k - 1], recv_sem=s_recv.at[k - 1],
-            device_id=(my_dp, b), device_id_type=MESH,
-        )
-        copy.start()
-        early.append(copy)
-
-    for copy in sends:
-        copy.wait_recv()
+    for k in reversed(range(1, MP)):
+        pltpu.make_async_remote_copy(
+            src_ref=sq.at[mp_peers[k]], dst_ref=sq_slots.at[k - 1], send_sem=s_send, recv_sem=s_recv,
+            device_id=(my_dp, mp_peers[k]), device_id_type=MESH,
+        ).start()
+
+    drain(ch_slots, a_recv)
     ch4 = ch_buf[...].astype(f32)
     for d in range(DP - 1):
         ch4 = ch4 + ch_slots[d].astype(f32)
@@ -147,14 +146,11 @@
         norms = jnp.where(lane1 == t, nh[t:t + 1], norms)
         norms = jnp.where(lane1 == STEPS + t, na[t:t + 1], norms)
     norm_buf[...] = norms
-    for k, b in order:
-        copy = pltpu.make_async_remote_copy(
-            src_ref=norm_buf, dst_ref=norm_slots.at[k - 1],
-            send_sem=n_send.at[k - 1], recv_sem=n_recv.at[k - 1],
-            device_id=(my_dp, b), device_id_type=MESH,
-        )
-        copy.start()
-        early.append(copy)
+    for k in reversed(range(1, MP)):
+        pltpu.make_async_remote_copy(
+            src_ref=norm_buf, dst_ref=norm_slots.at[k - 1], send_sem=n_send, recv_sem=n_recv,
+            device_id=(my_dp, mp_peers[k]), device_id_type=MESH,
+        ).start()
     cols = cm.T
     id_cols, v_cols = [], []
     for t in range(STEPS):
@@ -163,8 +159,8 @@
         id_cols.append(code.astype(jnp.int32))
         v_cols.append(col[3 * depth:])
 
-    outs = []
-    for d, b in order + [(0, my_mp)]:
+    for k in reversed(range(MP)):
+        b = mp_peers[k]
         hb = h[pl.ds(b * (blk // tall), blk // tall)].reshape(blk, width)
         hh = lax.dot_general(ch, hb, NT, preferred_element_type=f32)
         part[b, 0:STEPS] = hh[0:STEPS]
@@ -178,48 +174,48 @@
                 part[b, STEPS + t:STEPS + t + 1, j * LANES:(j + 1) * LANES] = jnp.sum(
                     bv * w, axis=0, keepdims=True
                 )
-        if d:
-            copy = pltpu.make_async_remote_copy(
-                src_ref=part.at[b], dst_ref=part_slots.at[d - 1],
-                send_sem=b_send.at[d - 1], recv_sem=b_recv.at[d - 1],
+        if k:
+            pltpu.make_async_remote_copy(
+                src_ref=part.at[b], dst_ref=part_slots.at[k - 1], send_sem=b_send, recv_sem=b_recv,
                 device_id=(my_dp, b), device_id_type=MESH,
-            )
-            copy.start()
-            outs.append(copy)
-    own, norms, total = sq[my_mp], norm_buf[...], part[my_mp]
-    for copy in early + outs:
-        copy.wait_recv()
+            ).start()
+    own, norms = sq[my_mp], norm_buf[...]
+    drain(sq_slots, s_recv)
+    drain(norm_slots, n_recv)
     for k in range(MP - 1):
         own = own + sq_slots[k]
         norms = norms + norm_slots[k]
+    own = own[0:1] * own[1:2]
+    bases = [own + norms[:, t:t + 1] * norms[:, STEPS + t:STEPS + t + 1] for t in range(STEPS)]
+    total = part[my_mp]
+    drain(part_slots, b_recv)
+    for k in range(MP - 1):
         total = total + part_slots[k]
-
-    own = own[0:1] * own[1:2]
     row = jnp.zeros((1, LANES), f32)
     low = None
     for t in range(STEPS):
-        center = norms[:, t:t + 1] * norms[:, STEPS + t:STEPS + t + 1]
         cross = total[t:t + 1] * total[STEPS + t:STEPS + t + 1]
-        dist = jnp.maximum(own + center - 2.0 * cross, 0.0)
+        dist = jnp.maximum(bases[t] - 2.0 * cross, 0.0)
         low = dist if low is None else jnp.minimum(low, dist)
         row = jnp.where(lane1 == t, jnp.sum(low, axis=1, keepdims=True), row)
     row_buf[...] = row
-    lasts = []
-    for d in range(1, DP * MP):
-        to = lax.rem(me + d, DP * MP)
-        copy = pltpu.make_async_remote_copy(
-            src_ref=row_buf, dst_ref=row_slots.at[pl.ds(me, 1)],
-            send_sem=d_send.at[d - 1], recv_sem=d_recv.at[d - 1],
-            device_id=(lax.div(to, MP), lax.rem(to, MP)), device_id_type=MESH,
-        )
-        copy.start()
-        lasts.append(copy)
+    for kd in reversed(range(DP)):
+        for km in reversed(range(MP)):
+            if kd or km:
+                pltpu.make_async_remote_copy(
+                    src_ref=row_buf, dst_ref=row_slots.at[pl.ds(me, 1)],
+                    send_sem=d_send, recv_sem=d_recv,
+                    device_id=(dp_peers[kd], mp_peers[km]), device_id_type=MESH,
+                ).start()
     row_slots[pl.ds(me, 1), :] = row
     dist_ref[...] = low
-    for copy in sends + early + outs:
-        copy.wait_send()
-    for copy in lasts:
-        copy.wait()
+    drain(ch_slots, a_send)
+    drain(sq_slots, s_send)
+    drain(norm_slots, n_send)
+    drain(part_slots, b_send)
+    others = row_slots.at[pl.ds(0, DP * MP - 1)]
+    drain(others, d_send)
+    drain(others, d_recv)
     mean_ref[...] = jnp.sum(row_slots[...], axis=0, keepdims=True) / (blk * MP * DP)
 
 
@@ -253,12 +249,7 @@
                 vm((MP - 1, 2 * STEPS, blk), jnp.float32),
                 vm((1, LANES), jnp.float32),
                 vm((DP * MP, LANES), jnp.float32),
-                sem, sem, sem((rows // LANES,)), sem((rows // LANES,)),
-                sem((DP - 1,)), sem((DP - 1,)),
-                sem((MP - 1,)), sem((MP - 1,)),
-                sem((MP - 1,)), sem((MP - 1,)),
-                sem((MP - 1,)), sem((MP - 1,)),
-                sem((DP * MP - 1,)), sem((DP * MP - 1,)),
+                *[sem] * 14,
             ],
             compiler_params=pltpu.CompilerParams(collective_id=0, has_side_effects=True),
         )(centers, hidden_states.reshape(rows // TALL, TALL, width), factor_values.T, class_ids.T)

time: 20.5 us -> 19.5 us (0.951)
  Pallas kernels: 18.7 us -> 17.6 us
    pallas_call x1, Pallas kernels: 18.7 us -> 17.6 us  [body(): pl.pallas_call(functools.partial(kernel, DP, MP), out_shape=(vm((1, blk),...]
where the time goes in v3:
time: 19.5 us; the launch traced here: 19.3 us
  Pallas kernels  17.6 us (90%)
  local copies, waits for them, and re-layouts  1.09 us (6%)
  between operations  0.64 us (3%)
    pallas_call x1, Pallas kernels, body(): pl.pallas_call(functools.partial(kernel, DP, MP), out_shape=(vm((1, blk),...  17.6 us
    unnamed x1, local copies, waits for them, and re-layouts  0.58 us
    squeeze x1, local copies, waits for them, and re-layouts, body(): return (low.reshape(blk), mean[0, :STEPS])  0.51 us

profile of v3, /device:TPU:0, one launch (start us, length us, event | category | flops | bytes accessed | tf_op | source)
XLA Modules:
  0.0 19.3 jit_solution(4334752543122298220)
XLA Ops:
  0.6 17.6 %shard_map.59 = (f32[1,512]{1,0:T(1,128)S(1)}, f32[1,128]{1,0:T(1,128)S(1)}) custom-call(s32[3]{0:T(128)} %c_hbm.1, bf16[128,16,1024]{2,1,0:T(8,128)(2,1)} %bitcast.7, bf16[16,2048]{1,0:T(8,128)(2,1)} %bitcast.9, s32[16,2048]{1,0:T(8,128)} %bitcast.8), custom_call_target="tpu_custom_call" | custom-call | tf_op jit(solution)/shard_map/pallas_call | solution.py:232
  18.2 0.6 %copy.7 = f32[512]{0:T(512)} copy(f32[512]{0:T(512)S(1)} %bitcast.6) | data formatting | bytes 4096
  18.8 0.5 %slice_bitcast_fusion = f32[3]{0:T(128)} fusion(f32[1,128]{1,0:T(1,128)S(1)} %get-tuple-element.5), kind=kLoop, calls=%fused_computation | loop fusion | bytes 24 | tf_op jit(solution)/shard_map/squeeze | solution.py:256

commit v4 on v3

--- a/solution.py
+++ b/solution.py
@@ -29,6 +29,11 @@
 
 def drain(ref, sem):
     pltpu.make_async_copy(ref, ref, sem).wait()
+
+
+def finish(low_ref, mean_ref, dist_ref, means_ref):
+    dist_ref[...] = low_ref[...]
+    means_ref[...] = mean_ref[0:STEPS]
 
 
 def kernel(
@@ -253,7 +258,19 @@
             ],
             compiler_params=pltpu.CompilerParams(collective_id=0, has_side_effects=True),
         )(centers, hidden_states.reshape(rows // TALL, TALL, width), factor_values.T, class_ids.T)
-        return low.reshape(blk), mean[0, :STEPS]
+        spec = pl.BlockSpec(memory_space=vm)
+        return pl.pallas_call(
+            finish,
+            out_shape=(
+                jax.ShapeDtypeStruct((blk,), jnp.float32),
+                jax.ShapeDtypeStruct((STEPS,), jnp.float32),
+            ),
+            in_specs=[spec, spec],
+            out_specs=(spec, spec),
+        )(
+            pltpu.with_memory_space_constraint(low.reshape(blk), vm),
+            pltpu.with_memory_space_constraint(mean.reshape(LANES), vm),
+        )
 
     return jax.shard_map(
         body,

time: 19.5 us -> 19 us (0.974)
  local copies, waits for them, and re-layouts: 1.09 us -> 0 us
  Pallas kernels: 17.6 us -> 18.2 us
    pallas_call x0 -> x1, Pallas kernels: none -> 0.58 us  [body(): pl.pallas_call(finish, out_shape=(jax.ShapeDtypeStruct((blk,), jnp.float3...]
    unnamed x1 -> x0, local copies, waits for them, and re-layouts: 0.58 us -> none
    squeeze x1 -> x0, local copies, waits for them, and re-layouts: 0.51 us -> none  [body(): return (low.reshape(blk), mean[0, :STEPS])]
where the time goes in v4:
time: 19 us; the launch traced here: 18.8 us
  Pallas kernels  18.2 us (96%)
  between operations  0.64 us (3%)
    pallas_call x1, Pallas kernels, body(): pl.pallas_call(functools.partial(kernel, DP, MP), out_shape=(vm((1, blk),...  17.6 us
    pallas_call x1, Pallas kernels, body(): pl.pallas_call(finish, out_shape=(jax.ShapeDtypeStruct((blk,), jnp.float3...  0.58 us

profile of v4, /device:TPU:0, one launch (start us, length us, event | category | flops | bytes accessed | tf_op | source)
XLA Modules:
  0.0 18.8 jit_solution(11186545912117192130)
XLA Ops:
  0.6 17.6 %shard_map.59 = (f32[1,512]{1,0:T(1,128)S(1)}, f32[1,128]{1,0:T(1,128)S(1)}) custom-call(s32[3]{0:T(128)} %c_hbm.1, bf16[128,16,1024]{2,1,0:T(8,128)(2,1)} %bitcast.7, bf16[16,2048]{1,0:T(8,128)(2,1)} %bitcast.9, s32[16,2048]{1,0:T(8,128)} %bitcast.8), custom_call_target="tpu_custom_call" | custom-call | tf_op jit(solution)/shard_map/pallas_call | solution.py:237
  18.2 0.6 %shard_map.60 = (f32[512]{0:T(512)}, f32[3]{0:T(128)}) custom-call(f32[512]{0:T(512)S(1)} %bitcast.5, f32[128]{0:T(128)S(1)} %bitcast.6), custom_call_target="tpu_custom_call" | custom-call | tf_op jit(solution)/shard_map/pallas_call | solution.py:262
